TPU v7x, 32 devices: a whole 2x2x4 slice. The times are simulated.
32 devices in a mesh: dp: 8 (over y, x, core), fsdp: 4 (over z).
Axes of the slice: x: 2, y: 2, z: 4, core: 2. Of those that a mesh axis runs over, the one named last changes fastest.
Arguments:
- tokens: bfloat16 [4096, 4096], P('dp'), may hold values from -6 to 6
- counts: int32 [8], P('dp'), may hold values from 256 to 512, as said below
- patch_index: int32 [4096], P('dp'), may hold values from 0 to 255
- clip_limit: float32 [], replicated, may hold values from 1024 to 8192
- norm_gain: float32 [4, 4096], replicated, may hold values from 0.25 to 1.75
- params: float32 [4, 4096, 4096], P(None, 'dp', 'fsdp'), may hold values from -0.09375 to 0.09375
- moments: float32 [4, 4096, 4096], P(None, 'dp', 'fsdp'), may hold values from -0.3 to 0.3
- seconds: float32 [4, 4096, 4096], P(None, 'dp', 'fsdp'), may hold values from 0.05 to 1
- gradients: float32 [4, 4096, 4096], P(None, 'dp', 'fsdp'), may hold values from -48 to 48
Outputs:
- params_new: float32 [4, 4096, 4096], P(None, 'dp', 'fsdp')
- moments_new: float32 [4, 4096, 4096], P(None, 'dp', 'fsdp')
- seconds_new: float32 [4, 4096, 4096], P(None, 'dp', 'fsdp')
- mixed: bfloat16 [4096, 4096], P('dp', 'fsdp')
Inputs may be any that keep to these rules, and one draw needn't show every extreme that they name: `counts`: at most 512, reached on some index of dp in every draw.
All inputs are finite; a program needn't handle non-finite values.
Results may differ from a plain program's by a relative error of at most 0.0095.
Values may be sent and summed in bfloat16 or wider, within the bound.
A program may use at most 192 MiB of HBM per device.

v0:
```python
import jax
import jax.numpy as jnp
from jax import lax
from jax.sharding import PartitionSpec as P

D = 4096
LAYERS = 4
GRID = 16
STEP = 40
beta_one = 0.9
beta_two = 0.95
adam_eps = 1e-08
learning_rate = 0.0024
weight_decay = 0.05
norm_eps = 1e-06


def position_code(patch_index):
    quarter = D // 4
    freqs = 1.0 / 10000.0 ** (jnp.arange(quarter, dtype=jnp.float32) / quarter)
    across = (patch_index // GRID).astype(jnp.float32)[:, None] * freqs[None, :]
    downward = (patch_index % GRID).astype(jnp.float32)[:, None] * freqs[None, :]
    return jnp.concatenate(
        [jnp.sin(across), jnp.cos(across), jnp.sin(downward), jnp.cos(downward)], axis=1
    )


def layer_norm(stream, gain_row):
    centre = jnp.mean(stream, axis=1, keepdims=True)
    shifted = stream - centre
    spread = jnp.mean(shifted * shifted, axis=1, keepdims=True)
    return (shifted * lax.rsqrt(spread + norm_eps) * gain_row[None, :]).astype(jnp.bfloat16)


def adam_update(params, moments, seconds, gradients, factor):
    clipped = gradients * factor
    moments_new = beta_one * moments + (1.0 - beta_one) * clipped
    seconds_new = beta_two * seconds + (1.0 - beta_two) * clipped * clipped
    direction = (
        moments_new
        / (1.0 - beta_one**STEP)
        / (jnp.sqrt(seconds_new / (1.0 - beta_two**STEP)) + adam_eps)
    )
    params_new = params - learning_rate * (direction + weight_decay * params)
    return (params_new, moments_new, seconds_new)


def advance(stream, branch, current, col_first, col_count):
    if current + 1 < LAYERS:
        widened = lax.all_gather(branch, "fsdp", axis=1, tiled=True)
        return stream + widened.astype(jnp.float32)
    return lax.dynamic_slice_in_dim(stream, col_first, col_count, 1) + branch.astype(jnp.float32)


def per_device(
    tokens, counts, patch_index, clip_limit, norm_gain, params, moments, seconds, gradients
):
    squares = lax.psum(jnp.sum(gradients * gradients), ("dp", "fsdp"))
    factor = jnp.minimum(1.0, clip_limit / (jnp.sqrt(squares) + 1e-06))
    params_new, moments_new, seconds_new = adam_update(params, moments, seconds, gradients, factor)
    weights = params_new.astype(jnp.bfloat16)
    tok_rows = tokens.shape[0]
    col_count = weights.shape[2]
    col_first = lax.axis_index("fsdp") * col_count
    valid = lax.broadcasted_iota(jnp.int32, (tok_rows, 1), 0) < counts[0]
    stream = jnp.where(valid, tokens.astype(jnp.float32) + position_code(patch_index), 0.0)
    gathered = lax.all_gather(weights, "dp", axis=1, tiled=True)
    for current in range(LAYERS):
        normed = layer_norm(stream, norm_gain[current])
        branch = jnp.dot(normed, gathered[current], preferred_element_type=jnp.float32).astype(
            jnp.bfloat16
        )
        stream = advance(stream, branch, current, col_first, col_count)
    mixed = jnp.where(valid, stream, 0.0).astype(jnp.bfloat16)
    return (params_new, moments_new, seconds_new, mixed)


def solution(mesh):
    in_specs = (
        P("dp", None),
        P("dp"),
        P("dp"),
        P(),
        P(),
        P(None, "dp", "fsdp"),
        P(None, "dp", "fsdp"),
        P(None, "dp", "fsdp"),
        P(None, "dp", "fsdp"),
    )
    out_specs = (
        P(None, "dp", "fsdp"),
        P(None, "dp", "fsdp"),
        P(None, "dp", "fsdp"),
        P("dp", "fsdp"),
    )
    return jax.shard_map(
        per_device, mesh=mesh, in_specs=in_specs, out_specs=out_specs, check_vma=False
    )
```

profile of v0, /device:TPU:0, one launch (start us, length us, event | category | flops | bytes accessed | tf_op | source)
XLA Modules:
  0.0 556.9 jit_solution(18285389573598532073)
XLA Ops:
  7.2 6.1 %multiply_reduce_fusion.4 = f32[]{:T(128)} fusion(f32[4,512,1024]{2,1,0:T(8,128)} %param.17), kind=kLoop, calls=%fused_computation.25 | loop fusion | flops 4194303 | bytes 8388612 | tf_op jit(solution)/shard_map/reduce_sum | solution.py:58
  14.0 42.2 %psum.7 = f32[]{:T(128)} all-reduce(f32[]{:T(128)} %multiply_reduce_fusion.4), channel_id=1, replica_groups=mesh['dp'=8,'fsdp'=4] {'dp','fsdp'}, use_global_device_ids=true, to_apply=%region_1.0 | all-reduce | flops 1 | bytes 8 | tf_op jit(solution)/shard_map/psum | solution.py:58
  57.0 20.8 %fusion.30 = (bf16[4,512,1024]{2,1,0:T(8,128)(2,1)}, f32[4,512,1024]{2,1,0:T(8,128)}, f32[4,512,1024]{2,1,0:T(8,128)}, f32[4,512,1024]{2,1,0:T(8,128)}) fusion(f32[4,512,1024]{2,1,0:T(8,128)} %param.14, f32[4,512,1024]{2,1,0:T(8,128)} %param.17, f32[]{:T(128)S(6)} %min.3, f32[4,512,1024]{2,1,0:T(8,128)} %param.15, f32[4,512,1024]{2,1,0:T(8,128)} %param.16), kind=kLoop, calls=%fused_computation.71 | loop fusion | flops 35651584 | bytes 62914564 | tf_op jit(solution)/shard_map/convert_element_type | solution.py:61
  77.8 0.2 all-gather.7.cloned.1.call-start
  78.9 14.7 %multiply_sine_fusion.1 = (f32[512,1024]{1,0:T(8,128)S(1)}, f32[512,1024]{1,0:T(8,128)S(1)}, f32[512,1024]{1,0:T(8,128)S(1)}, f32[512,1024]{1,0:T(8,128)S(1)}) fusion(f32[1024]{0:T(1024)S(1)} %negate_power_fusion, f32[512]{0:T(512)S(1)} %get-tuple-element.24, f32[512]{0:T(512)S(1)} %get-tuple-element.25), kind=kLoop, calls=%fused_computation.41 | loop fusion | flops 1048576 | bytes 8396800 | tf_op jit(solution)/shard_map/sin | solution.py:24
  93.7 1.7 fusion.28
  95.4 3.2 copy-done
  98.6 1.0 multiply_reduce_fusion.3
  99.6 139.0 %all-gather.5.cloned.1.call-done = bf16[4,4096,1024]{2,1,0:T(8,128)(2,1)} async-done(((bf16[4,512,1024]{2,1,0:T(8,128)(2,1)}), bf16[4,4096,1024]{2,1,0:T(8,128)(2,1)}) %all-gather.5.cloned.1.call-update) | async-done | bytes 33554448 | tf_op jit(solution)/shard_map/all_gather | solution.py:67
  238.6 11.3 %fusion.18 = bf16[512,1024]{1,0:T(8,128)(2,1)} fusion(bf16[4,4096,1024]{2,1,0:T(8,128)(2,1)} %all-gather.5.cloned.1.call-done, f32[512,4096]{1,0:T(8,128)} %copy-done, f32[4096]{0:T(1024)S(1)} %bitcast.33, f32[512]{0:T(512)S(1)} %add_rsqrt_fusion.3, f32[512]{0:T(512)S(1)} %broadcast_multiply_fusion.3), kind=kOutput, calls=%fused_computation.43 | convolution fusion | flops 4303880192 | bytes 17846272 | tf_op jit(solution)/shard_map/dot_general | solution.py:70
  250.0 80.8 %all-gather.7.cloned.1.call-done = bf16[512,4096]{1,0:T(8,128)(2,1)} async-done(((bf16[512,1024]{1,0:T(8,128)(2,1)}), bf16[512,4096]{1,0:T(8,128)(2,1)}) %all-gather.7.cloned.1.call-update) | async-done | bytes 4194320 | tf_op jit(solution)/shard_map/all_gather | solution.py:50
  330.8 5.6 %fusion.22 = f32[512]{0:T(512)S(1)} fusion(f32[512,4096]{1,0:T(8,128)} %copy-done, bf16[512,4096]{1,0:T(8,128)(2,1)} %all-gather.7.cloned.1.call-done), kind=kLoop, calls=%fused_computation.47 | loop fusion | flops 6290944 | bytes 12584960 | tf_op jit(solution)/shard_map/reduce_sum | solution.py:29
  336.6 5.2 multiply_reduce_fusion.2
  341.8 9.2 %fusion.19 = bf16[512,1024]{1,0:T(8,128)(2,1)} fusion(bf16[4,4096,1024]{2,1,0:T(8,128)(2,1)} %all-gather.5.cloned.1.call-done, f32[4096]{0:T(1024)S(1)} %bitcast.32, f32[512]{0:T(512)S(1)} %add_rsqrt_fusion.2, f32[512]{0:T(512)S(1)} %broadcast_multiply_fusion.2, f32[512,4096]{1,0:T(8,128)S(1)} %bitcast.29, bf16[512,4096]{1,0:T(8,128)(2,1)S(1)} %copy-done.2), kind=kOutput, calls=%fused_computation.44 | convolution fusion | flops 4308074496 | bytes 22040576 | tf_op jit(solution)/shard_map/dot_general | solution.py:70
  351.1 0.3 all-gather.11.cloned.1.call-start
  351.4 79.1 %all-gather.9.cloned.1.call-done = bf16[512,4096]{1,0:T(8,128)(2,1)} async-done(((bf16[512,1024]{1,0:T(8,128)(2,1)}), bf16[512,4096]{1,0:T(8,128)(2,1)}) %all-gather.9.cloned.1.call-update) | async-done | bytes 4194320 | tf_op jit(solution)/shard_map/all_gather | solution.py:50
  430.4 10.3 %fusion.27 = (f32[512]{0:T(512)S(1)}, f32[512,4096]{1,0:T(8,128)}) fusion(bf16[512,4096]{1,0:T(8,128)(2,1)} %all-gather.9.cloned.1.call-done, f32[512,4096]{1,0:T(8,128)} %copy-done, bf16[512,4096]{1,0:T(8,128)(2,1)} %all-gather.7.cloned.1.call-done), kind=kLoop, calls=%fused_computation.69 | loop fusion | flops 10485248 | bytes 25167872 | tf_op jit(solution)/shard_map/reduce_sum | solution.py:29
  440.8 4.5 multiply_reduce_fusion.1
  445.3 1.3 copy-done.1
  446.5 9.0 %fusion.20 = bf16[512,1024]{1,0:T(8,128)(2,1)} fusion(bf16[4,4096,1024]{2,1,0:T(8,128)(2,1)} %all-gather.5.cloned.1.call-done, f32[512,4096]{1,0:T(8,128)S(1)} %copy-done.1, f32[4096]{0:T(1024)S(1)} %bitcast.31, f32[512]{0:T(512)S(1)} %add_rsqrt_fusion.1, f32[512]{0:T(512)S(1)} %broadcast_multiply_fusion.1), kind=kOutput, calls=%fused_computation.45 | convolution fusion | flops 4303880192 | bytes 17846272 | tf_op jit(solution)/shard_map/dot_general | solution.py:70
  455.6 79.4 %all-gather.11.cloned.1.call-done = bf16[512,4096]{1,0:T(8,128)(2,1)} async-done(((bf16[512,1024]{1,0:T(8,128)(2,1)}), bf16[512,4096]{1,0:T(8,128)(2,1)}) %all-gather.11.cloned.1.call-update) | async-done | bytes 4194320 | tf_op jit(solution)/shard_map/all_gather | solution.py:50
  535.0 5.5 fusion.26
  540.5 1.0 multiply_reduce_fusion
  541.4 8.9 %select_convert_fusion = bf16[512,1024]{1,0:T(8,128)(2,1)} fusion(f32[512,4096]{1,0:T(8,128)S(1)} %get-tuple-element.5, s32[]{:T(128)S(6)} %select_n.26, bf16[4,4096,1024]{2,1,0:T(8,128)(2,1)} %all-gather.5.cloned.1.call-done, f32[4096]{0:T(1024)S(1)} %bitcast.30, f32[512]{0:T(512)S(1)} %add_rsqrt_fusion, f32[512]{0:T(512)S(1)} %broadcast_multiply_fusion, ...), kind=kOutput, calls=%fused_computation.42 | convolution fusion | flops 4305977344 | bytes 19943940 | tf_op jit(solution)/shard_map/dot_general | solution.py:70
  (33 shorter events, 0.4 us)
Async XLA Ops:
  7.2 231.5 %all-gather.5.cloned.1.call-start = ((), (), s32[]{:S(2)}) async-start(), calls=%async_computation | async-start | bytes 37748736 | tf_op jit(solution)/shard_map/all_gather | solution.py:67
  57.0 21.9 %copy-start.5 = (s32[512]{0:T(512)S(1)}, s32[512]{0:T(512)}, u32[]{:S(2)}) copy-start(s32[512]{0:T(512)} %param.11) | copy-start | bytes 6148
  77.8 253.0 %all-gather.7.cloned.1.call-start = ((), (), s32[]{:S(2)}) async-start(), calls=%async_computation.1 | async-start | bytes 5242880 | tf_op jit(solution)/shard_map/all_gather | solution.py:50
  78.0 15.6 %copy-start.3 = (bf16[512,4096]{1,0:T(8,128)(2,1)S(1)}, bf16[512,4096]{1,0:T(8,128)(2,1)}, u32[]{:S(2)}) copy-start(bf16[512,4096]{1,0:T(8,128)(2,1)} %param.9) | copy-start | bytes 12582916
  95.4 3.2 copy-start
  95.4 4.2 copy-start.4
  249.9 180.5 %all-gather.9.cloned.1.call-start = ((), (), s32[]{:S(2)}) async-start(), calls=%async_computation.2 | async-start | bytes 5242880 | tf_op jit(solution)/shard_map/all_gather | solution.py:50
  330.8 5.8 %copy-start.2 = (bf16[512,4096]{1,0:T(8,128)(2,1)S(1)}, bf16[512,4096]{1,0:T(8,128)(2,1)}, u32[]{:S(2)}) copy-start(bf16[512,4096]{1,0:T(8,128)(2,1)} %all-gather.7.cloned.1.call-done) | copy-start | bytes 12582916
  330.8 11.0 %slice-start = ((s8[8388608]{0:T(1024)(128)(4,1)}), s8[4194304]{0:T(1024)(128)(4,1)S(1)}, s32[]{:S(2)}) async-start(s8[8388608]{0:T(1024)(128)(4,1)} %bitcast.28), calls=%async_computation.4 | async-start | bytes 8388608
  336.6 5.2 slice-start.1
  351.1 183.9 %all-gather.11.cloned.1.call-start = ((), (), s32[]{:S(2)}) async-start(), calls=%async_computation.3 | async-start | bytes 5242880 | tf_op jit(solution)/shard_map/all_gather | solution.py:50
  440.7 5.8 %copy-start.1 = (f32[512,4096]{1,0:T(8,128)S(1)}, f32[512,4096]{1,0:T(8,128)}, u32[]{:S(2)}) copy-start(f32[512,4096]{1,0:T(8,128)} %get-tuple-element.7) | copy-start | bytes 25165828
Sparse Core Ops, SparseCore 0:
  77.9 160.6 all-gather.4
  250.0 80.7 all-gather.6
  351.2 79.2 all-gather.8
  455.7 79.2 all-gather.10
where the time goes:
time: 557 us
  waiting for transfers between devices  378 us (68%)
  other arithmetic  76.5 us (14%)
  blocking collectives  42.2 us (8%)
  matrix products  38.4 us (7%)
  between operations  16.1 us (3%)
    all_gather x3, waiting for transfers between devices, advance(): widened = lax.all_gather(branch, 'fsdp', axis=1, tiled=True)  239 us
    all_gather x1, waiting for transfers between devices, per_device(): gathered = lax.all_gather(weights, 'dp', axis=1, tiled=True)  139 us
    psum x1, blocking collectives, per_device(): squares = lax.psum(jnp.sum(gradients * gradients), ('dp', 'fsdp'))  42.2 us
    dot_general x4, matrix products, per_device(): jnp.dot(normed, gathered[current], preferred_element_type=jnp.float32)  38.4 us
    reduce_sum x4, other arithmetic, layer_norm(): centre = jnp.mean(stream, axis=1, keepdims=True)  23.1 us
    convert_element_type x1, other arithmetic, per_device(): weights = params_new.astype(jnp.bfloat16)  20.8 us
    sin x1, other arithmetic, position_code(): jnp.sin(across)  14.7 us
    reduce_sum x4, other arithmetic, layer_norm(): spread = jnp.mean(shifted * shifted, axis=1, keepdims=True)  11.6 us
  transfers between devices with their start and end apart: 4, of which 4 were waited for; matrix products, arithmetic and copies ran while one was open for 3% of the time, Pallas kernels for 0%

commit v1 on v0

--- a/solution.py
+++ b/solution.py
@@ -47,7 +47,8 @@
 
 def advance(stream, branch, current, col_first, col_count):
     if current + 1 < LAYERS:
-        widened = lax.all_gather(branch, "fsdp", axis=1, tiled=True)
+        shards = lax.all_gather(branch, "fsdp", axis=0, tiled=False)
+        widened = jnp.concatenate(shards, axis=1)
         return stream + widened.astype(jnp.float32)
     return lax.dynamic_slice_in_dim(stream, col_first, col_count, 1) + branch.astype(jnp.float32)
 

time: 557 us -> 596 us (1.070)
  other arithmetic: 76.5 us -> 96.9 us
  local copies, waits for them, and re-layouts: 4.64 us -> 19.2 us
    convert_element_type x0 -> x3, local copies, waits for them, and re-layouts: none -> 12.1 us  [advance(): return stream + widened.astype(jnp.float32)]
    unnamed x1 -> x3, other arithmetic: 0.01 us -> 9.64 us
    reduce_sum x4, other arithmetic: 23.1 us -> 31 us  [layer_norm(): centre = jnp.mean(stream, axis=1, keepdims=True)]
where the time goes in v1:
time: 596 us; the launch traced here: 592 us
  waiting for transfers between devices  378 us (63%)
  other arithmetic  96.9 us (16%)
  blocking collectives  42.2 us (7%)
  matrix products  38.5 us (6%)
  local copies, waits for them, and re-layouts  19.2 us (3%)
  between operations  16.3 us (3%)
    all_gather x3, waiting for transfers between devices, advance(): shards = lax.all_gather(branch, 'fsdp', axis=0, tiled=False)  239 us
    all_gather x1, waiting for transfers between devices, per_device(): gathered = lax.all_gather(weights, 'dp', axis=1, tiled=True)  139 us
    psum x1, blocking collectives, per_device(): squares = lax.psum(jnp.sum(gradients * gradients), ('dp', 'fsdp'))  42.2 us
    dot_general x4, matrix products, per_device(): jnp.dot(normed, gathered[current], preferred_element_type=jnp.float32)  38.5 us
    reduce_sum x4, other arithmetic, layer_norm(): centre = jnp.mean(stream, axis=1, keepdims=True)  31 us
    convert_element_type x1, other arithmetic, per_device(): weights = params_new.astype(jnp.bfloat16)  20.9 us
    sin x1, other arithmetic, position_code(): jnp.sin(across)  14.7 us
    reduce_sum x4, other arithmetic, layer_norm(): spread = jnp.mean(shifted * shifted, axis=1, keepdims=True)  14.4 us
  transfers between devices with their start and end apart: 4, of which 4 were waited for; matrix products, arithmetic and copies ran while one was open for 3% of the time, Pallas kernels for 0%

profile of v1, /device:TPU:0, one launch (start us, length us, event | category | flops | bytes accessed | tf_op | source)
XLA Modules:
  0.0 592.1 jit_solution(1253583413773540594)
XLA Ops:
  7.2 6.1 %multiply_reduce_fusion.4 = f32[]{:T(128)} fusion(f32[4,512,1024]{2,1,0:T(8,128)} %param.17), kind=kLoop, calls=%fused_computation.25 | loop fusion | flops 4194303 | bytes 8388612 | tf_op jit(solution)/shard_map/reduce_sum | solution.py:59
  14.0 42.2 %psum.7 = f32[]{:T(128)} all-reduce(f32[]{:T(128)} %multiply_reduce_fusion.4), channel_id=1, replica_groups=mesh['dp'=8,'fsdp'=4] {'dp','fsdp'}, use_global_device_ids=true, to_apply=%region_1.0 | all-reduce | flops 1 | bytes 8 | tf_op jit(solution)/shard_map/psum | solution.py:59
  57.0 20.9 %fusion.30 = (bf16[4,512,1024]{2,1,0:T(8,128)(2,1)}, f32[4,512,1024]{2,1,0:T(8,128)}, f32[4,512,1024]{2,1,0:T(8,128)}, f32[4,512,1024]{2,1,0:T(8,128)}) fusion(f32[4,512,1024]{2,1,0:T(8,128)} %param.14, f32[4,512,1024]{2,1,0:T(8,128)} %param.17, f32[]{:T(128)S(6)} %min.3, f32[4,512,1024]{2,1,0:T(8,128)} %param.15, f32[4,512,1024]{2,1,0:T(8,128)} %param.16), kind=kLoop, calls=%fused_computation.71 | loop fusion | flops 35651584 | bytes 62914564 | tf_op jit(solution)/shard_map/convert_element_type | solution.py:62
  79.2 14.7 %multiply_sine_fusion.1 = (f32[512,1024]{1,0:T(8,128)S(1)}, f32[512,1024]{1,0:T(8,128)S(1)}, f32[512,1024]{1,0:T(8,128)S(1)}, f32[512,1024]{1,0:T(8,128)S(1)}) fusion(f32[1024]{0:T(1024)S(1)} %negate_power_fusion, f32[512]{0:T(512)S(1)} %get-tuple-element.26, f32[512]{0:T(512)S(1)} %get-tuple-element.27), kind=kLoop, calls=%fused_computation.41 | loop fusion | flops 1048576 | bytes 8396800 | tf_op jit(solution)/shard_map/sin | solution.py:24
  99.9 138.8 %all-gather.8.cloned.1.call-done = bf16[4,4096,1024]{2,1,0:T(8,128)(2,1)} async-done(((bf16[4,512,1024]{2,1,0:T(8,128)(2,1)}), bf16[4,4096,1024]{2,1,0:T(8,128)(2,1)}) %all-gather.8.cloned.1.call-update) | async-done | bytes 33554448 | tf_op jit(solution)/shard_map/all_gather | solution.py:68
  238.7 11.3 %fusion.18 = bf16[512,1024]{1,0:T(8,128)(2,1)} fusion(bf16[4,4096,1024]{2,1,0:T(8,128)(2,1)} %all-gather.8.cloned.1.call-done, f32[512,4096]{1,0:T(8,128)} %copy-done.1, f32[4096]{0:T(1024)S(1)} %bitcast.55, f32[512]{0:T(512)S(1)} %add_rsqrt_fusion.3, f32[512]{0:T(512)S(1)} %broadcast_multiply_fusion.3), kind=kOutput, calls=%fused_computation.43 | convolution fusion | flops 4303880192 | bytes 17846272 | tf_op jit(solution)/shard_map/dot_general | solution.py:71
  250.0 80.8 %all-gather.10.cloned.1.call-done = bf16[2048,1024]{1,0:T(8,128)(2,1)} async-done(((bf16[512,1024]{1,0:T(8,128)(2,1)}), bf16[2048,1024]{1,0:T(8,128)(2,1)}) %all-gather.10.cloned.1.call-update) | async-done | bytes 4194320 | tf_op jit(solution)/shard_map/all_gather | solution.py:50
  330.9 3.2 convert_bitcast_fusion.2
  334.1 4.1 copy.16
  338.2 9.8 %fusion.27 = (f32[512]{0:T(512)S(1)}, f32[512,4096]{1,0:T(8,128)}) fusion(f32[512,4096]{1,0:T(8,128)} %copy-done.1, f32[512,4096]{1,0:T(8,128)} %bitcast.46), kind=kLoop, calls=%fused_computation.69 | loop fusion | flops 4193792 | bytes 25167872 | tf_op jit(solution)/shard_map/reduce_sum | solution.py:29
  347.9 4.5 multiply_reduce_fusion.2
  353.7 9.1 %fusion.19 = bf16[512,1024]{1,0:T(8,128)(2,1)} fusion(bf16[4,4096,1024]{2,1,0:T(8,128)(2,1)} %all-gather.8.cloned.1.call-done, f32[512,4096]{1,0:T(8,128)S(1)} %copy-done.2, f32[4096]{0:T(1024)S(1)} %bitcast.54, f32[512]{0:T(512)S(1)} %add_rsqrt_fusion.2, f32[512]{0:T(512)S(1)} %broadcast_multiply_fusion.2), kind=kOutput, calls=%fused_computation.44 | convolution fusion | flops 4303880192 | bytes 17846272 | tf_op jit(solution)/shard_map/dot_general | solution.py:71
  363.0 79.1 %all-gather.12.cloned.1.call-done = bf16[2048,1024]{1,0:T(8,128)(2,1)} async-done(((bf16[512,1024]{1,0:T(8,128)(2,1)}), bf16[2048,1024]{1,0:T(8,128)(2,1)}) %all-gather.12.cloned.1.call-update) | async-done | bytes 4194320 | tf_op jit(solution)/shard_map/all_gather | solution.py:50
  442.2 3.2 convert_bitcast_fusion.1
  445.4 4.1 copy.17
  449.4 9.8 %fusion.26 = (f32[512]{0:T(512)S(1)}, f32[512,4096]{1,0:T(8,128)}) fusion(f32[512,4096]{1,0:T(8,128)} %get-tuple-element.9, f32[512,4096]{1,0:T(8,128)} %bitcast.47), kind=kLoop, calls=%fused_computation.68 | loop fusion | flops 4193792 | bytes 25167872 | tf_op jit(solution)/shard_map/reduce_sum | solution.py:29
  459.2 4.5 multiply_reduce_fusion.1
  465.0 9.1 %fusion.20 = bf16[512,1024]{1,0:T(8,128)(2,1)} fusion(bf16[4,4096,1024]{2,1,0:T(8,128)(2,1)} %all-gather.8.cloned.1.call-done, f32[512,4096]{1,0:T(8,128)S(1)} %copy-done, f32[4096]{0:T(1024)S(1)} %bitcast.53, f32[512]{0:T(512)S(1)} %add_rsqrt_fusion.1, f32[512]{0:T(512)S(1)} %broadcast_multiply_fusion.1), kind=kOutput, calls=%fused_computation.45 | convolution fusion | flops 4303880192 | bytes 17846272 | tf_op jit(solution)/shard_map/dot_general | solution.py:71
  474.1 79.4 %all-gather.14.cloned.1.call-done = bf16[2048,1024]{1,0:T(8,128)(2,1)} async-done(((bf16[512,1024]{1,0:T(8,128)(2,1)}), bf16[2048,1024]{1,0:T(8,128)(2,1)}) %all-gather.14.cloned.1.call-update) | async-done | bytes 4194320 | tf_op jit(solution)/shard_map/all_gather | solution.py:50
  553.4 3.2 convert_bitcast_fusion
  556.7 4.0 copy.18
  560.7 9.8 %fusion.25 = (f32[512]{0:T(512)S(1)}, f32[512,4096]{1,0:T(8,128)}) fusion(f32[512,4096]{1,0:T(8,128)} %get-tuple-element.7, f32[512,4096]{1,0:T(8,128)} %bitcast.48), kind=kLoop, calls=%fused_computation.67 | loop fusion | flops 4193792 | bytes 25167872 | tf_op jit(solution)/shard_map/reduce_sum | solution.py:29
  570.5 4.5 multiply_reduce_fusion
  576.3 9.1 %select_convert_fusion = bf16[512,1024]{1,0:T(8,128)(2,1)} fusion(f32[512,4096]{1,0:T(8,128)S(1)} %copy-done.3, s32[]{:T(128)S(6)} %select_n.26, bf16[4,4096,1024]{2,1,0:T(8,128)(2,1)} %all-gather.8.cloned.1.call-done, f32[4096]{0:T(1024)S(1)} %bitcast.52, f32[512]{0:T(512)S(1)} %add_rsqrt_fusion, f32[512]{0:T(512)S(1)} %broadcast_multiply_fusion, ...), kind=kOutput, calls=%fused_computation.42 | convolution fusion | flops 4305977344 | bytes 19943940 | tf_op jit(solution)/shard_map/dot_general | solution.py:71
  (36 shorter events, 10.6 us)
Async XLA Ops:
  7.2 231.5 %all-gather.8.cloned.1.call-start = ((), (), s32[]{:S(2)}) async-start(), calls=%async_computation | async-start | bytes 37748736 | tf_op jit(solution)/shard_map/all_gather | solution.py:68
  57.0 22.2 %copy-start.6 = (s32[512]{0:T(512)S(1)}, s32[512]{0:T(512)}, u32[]{:S(2)}) copy-start(s32[512]{0:T(512)} %param.11) | copy-start | bytes 6148
  77.9 253.0 %all-gather.10.cloned.1.call-start = ((), (), s32[]{:S(2)}) async-start(), calls=%async_computation.1 | async-start | bytes 5242880 | tf_op jit(solution)/shard_map/all_gather | solution.py:50
  78.4 15.6 %copy-start.4 = (bf16[512,4096]{1,0:T(8,128)(2,1)S(1)}, bf16[512,4096]{1,0:T(8,128)(2,1)}, u32[]{:S(2)}) copy-start(bf16[512,4096]{1,0:T(8,128)(2,1)} %param.9) | copy-start | bytes 12582916
  95.7 3.2 copy-start.1
  95.7 4.2 copy-start.5
  250.0 192.2 %all-gather.12.cloned.1.call-start = ((), (), s32[]{:S(2)}) async-start(), calls=%async_computation.2 | async-start | bytes 5242880 | tf_op jit(solution)/shard_map/all_gather | solution.py:50
  347.9 5.8 copy-start.2
  362.8 190.7 %all-gather.14.cloned.1.call-start = ((), (), s32[]{:S(2)}) async-start(), calls=%async_computation.3 | async-start | bytes 5242880 | tf_op jit(solution)/shard_map/all_gather | solution.py:50
  459.2 5.8 copy-start
  570.5 5.8 copy-start.3
Sparse Core Ops, SparseCore 0:
  78.0 160.6 all-gather.7
  250.1 80.7 all-gather.9
  362.9 79.2 all-gather.11
  474.2 79.2 all-gather.13
